TPU v7x, 32 devices: a whole 2x2x4 slice. The times are simulated.
32 devices in a mesh: dp: 2 (over y), expert: 8 (over z, x), etp: 2 (over core).
Axes of the slice: x: 2, y: 2, z: 4, core: 2. Of those that a mesh axis runs over, the one named last changes fastest.
Arguments:
- tokens: bfloat16 [1024, 4096], P(('dp', 'expert'), 'etp'), may hold values from -6 to 6
- expert_ids: int32 [1024, 8], P(('dp', 'expert')), may hold values from 0 to 15, all different within a row; in each aligned block of 64 rows (0 to 63, 64 to 127, ...) at most 48 rows name the same one
- combine: float32 [1024, 8], P(('dp', 'expert')), may hold values from 0.05 to 1
- gate_weight: bfloat16 [16, 4096, 1536], P('expert', 'dp', 'etp'), may hold values from -0.09375 to 0.09375
- up_weight: bfloat16 [16, 4096, 1536], P('expert', 'dp', 'etp'), may hold values from -0.09375 to 0.09375
- down_weight: bfloat16 [16, 1536, 4096], P('expert', 'etp', 'dp'), may hold values from -0.15625 to 0.15625
Outputs:
- mixed: bfloat16 [1024, 4096], P(('dp', 'expert'), 'etp')
Inputs may be any that keep to these rules, and one draw needn't show every extreme that they name: `expert_ids`: each row names 8 different experts. In the rows of one device (aligned blocks of 64 rows) no expert is named by more than 48 rows, a bound that some block reaches.
All inputs are finite; a program needn't handle non-finite values.
Results may differ from a plain program's by a relative error of at most 0.008.
Values may be sent and summed in bfloat16 or wider, within the bound.
A program may use at most 192 MiB of HBM per device.

v0:
```python
import jax
import jax.numpy as jnp
from jax import lax
from jax.sharding import PartitionSpec as P


def shards(tokens, expert_ids, combine, gate_weight, up_weight, down_weight):
    tok_rows, top_count = expert_ids.shape
    held_count = gate_weight.shape[0]
    groups = lax.axis_size("expert")
    experts = held_count * groups
    capacity = min(tok_rows, 3 * tok_rows * top_count // (2 * experts))
    slots_all = experts * capacity
    onehot = (expert_ids[:, :, None] == jnp.arange(experts, dtype=jnp.int32)[None, None, :]).astype(
        jnp.int32
    )
    flattened = onehot.reshape(tok_rows * top_count, experts)
    before = jnp.cumsum(flattened, axis=0) - flattened
    slot_index = jnp.sum(before * flattened, axis=1).reshape(tok_rows, top_count)
    target = expert_ids * capacity + slot_index
    matches = target[:, :, None] == jnp.arange(slots_all, dtype=jnp.int32)[None, None, :]
    picker = jnp.any(matches, axis=1).astype(jnp.bfloat16)
    weights_map = jnp.sum(jnp.where(matches, combine[:, :, None], 0.0), axis=1)
    gathered = lax.all_gather(tokens, "etp", axis=1, tiled=True)
    packed = jnp.einsum("ts,td->sd", picker, gathered, preferred_element_type=jnp.float32).astype(
        jnp.bfloat16
    )
    arrived = lax.all_to_all(
        packed.reshape(groups, held_count, capacity, gathered.shape[1]),
        "expert",
        split_axis=0,
        concat_axis=2,
        tiled=True,
    )
    inputs = arrived[0]
    gate_part = jnp.einsum(
        "erd,edf->erf",
        inputs,
        lax.all_gather(gate_weight, "dp", axis=1, tiled=True),
        preferred_element_type=jnp.float32,
    )
    up_part = jnp.einsum(
        "erd,edf->erf",
        inputs,
        lax.all_gather(up_weight, "dp", axis=1, tiled=True),
        preferred_element_type=jnp.float32,
    )
    hidden = (jax.nn.silu(gate_part) * up_part).astype(jnp.bfloat16)
    partial_value = jnp.einsum(
        "erf,efd->erd",
        hidden,
        lax.all_gather(down_weight, "dp", axis=2, tiled=True),
        preferred_element_type=jnp.float32,
    ).astype(jnp.bfloat16)
    partial_value = lax.optimization_barrier(partial_value)
    summed = lax.psum_scatter(
        partial_value.astype(jnp.float32).astype(jnp.bfloat16),
        "etp",
        scatter_dimension=2,
        tiled=True,
    )
    returned_rows = lax.all_to_all(summed[None], "expert", split_axis=2, concat_axis=0, tiled=True)
    returned_rows = returned_rows.reshape(slots_all, returned_rows.shape[3])
    weight_high = weights_map.astype(jnp.bfloat16)
    weight_low = (weights_map - weight_high.astype(jnp.float32)).astype(jnp.bfloat16)
    result = jnp.dot(weight_high, returned_rows, preferred_element_type=jnp.float32)
    result = result + jnp.dot(weight_low, returned_rows, preferred_element_type=jnp.float32)
    return result.astype(jnp.bfloat16)


def solution(mesh):
    placed = (
        P(("dp", "expert"), "etp"),
        P(("dp", "expert"), None),
        P(("dp", "expert"), None),
        P("expert", "dp", "etp"),
        P("expert", "dp", "etp"),
        P("expert", "etp", "dp"),
    )
    return jax.shard_map(
        shards, mesh=mesh, in_specs=placed, out_specs=P(("dp", "expert"), "etp"), check_vma=False
    )
```

profile of v0, /device:TPU:1, one launch (start us, length us, event | category | flops | bytes accessed | tf_op | source)
XLA Modules:
  0.0 597.7 jit_solution(10712536201870545837)
XLA Ops:
  6.5 0.7 all-gather.4.cloned.1.call-update
  7.3 0.7 all-gather.6.cloned.1.call-update
  8.0 0.1 copy.46
  8.1 0.1 eq.43
  8.2 0.1 eq.39
  8.3 1.2 reduce-window.6
  9.5 0.2 slice_reduce_fusion
  9.7 0.1 fusion.7
  9.8 0.1 reshape.32
  10.0 0.1 copy.50
  10.1 2.2 all_gather.12
  12.3 0.5 fusion.1
  12.8 4.5 convolution_convert_fusion.1
  17.3 7.3 %all-to-all-start = ((bf16[8,2,48,4096]{3,2,1,0:T(8,128)(2,1)}), bf16[8,2,48,4096]{3,2,1,0:T(8,128)(2,1)}, u32[]{:S(2)}, u32[]{:S(2)}) async-start(bf16[8,2,48,4096]{3,2,1,0:T(8,128)(2,1)} %bitcast.38), calls=%async_computation | async-start | bytes 12582912 | tf_op jit(solution)/shard_map/all_to_all | solution.py:28
  24.7 0.7 all-gather.8.cloned.1.call-update
  25.3 0.2 reduce-scatter.2.cloned.1.call-start
  25.6 136.7 %all-to-all-done = bf16[8,2,48,4096]{3,2,1,0:T(8,128)(2,1)} async-done(((bf16[8,2,48,4096]{3,2,1,0:T(8,128)(2,1)}), bf16[8,2,48,4096]{3,2,1,0:T(8,128)(2,1)}, u32[]{:S(2)}, u32[]{:S(2)}) %all-to-all-start) | async-done | bytes 6291488 | tf_op jit(solution)/shard_map/all_to_all | solution.py:28
  162.3 6.2 %copy.52 = bf16[1,2,8,48,4096]{4,3,2,1,0:T(8,128)(2,1)} copy(bf16[1,2,8,48,4096]{4,3,1,2,0:T(8,128)(2,1)} %bitcast.3) | data formatting | bytes 12582912 | tf_op jit(solution)/shard_map/all_to_all | solution.py:28
  168.6 12.5 %fusion.10 = f32[2,384,768]{2,1,0:T(8,128)S(1)} fusion(bf16[2,384,4096]{2,1,0:T(8,128)(2,1)} %bitcast.42, bf16[2,4096,768]{2,1,0:T(8,128)(2,1)} %all-gather.4.cloned.1.call-done), kind=kOutput, calls=%fused_computation.23 | convolution fusion | flops 4831838208 | bytes 21233664 | tf_op jit(solution)/shard_map/erd,edf->erf/dot_general | solution.py:36
  181.0 134.4 %all-gather.6.cloned.1.call-done = bf16[2,4096,768]{2,1,0:T(8,128)(2,1)} async-done(((bf16[2,2048,768]{2,1,0:T(8,128)(2,1)}), bf16[2,4096,768]{2,1,0:T(8,128)(2,1)}) %all-gather.6.cloned.1.call-update) | async-done | bytes 12582928 | tf_op jit(solution)/shard_map/all_gather | solution.py:45
  315.4 154.1 %all-gather.8.cloned.1.call-done = bf16[2,768,4096]{2,1,0:T(8,128)(2,1)} async-done(((bf16[2,768,2048]{2,1,0:T(8,128)(2,1)}), bf16[2,768,4096]{2,1,0:T(8,128)(2,1)}) %all-gather.8.cloned.1.call-update) | async-done | bytes 12582928 | tf_op jit(solution)/shard_map/all_gather | solution.py:52
  469.5 20.5 %convolution_convert_fusion = bf16[2,384,4096]{2,1,0:T(8,128)(2,1)} fusion(bf16[2,768,4096]{2,1,0:T(8,128)(2,1)} %all-gather.8.cloned.1.call-done, f32[2,384,768]{2,1,0:T(8,128)S(1)} %fusion.10, bf16[2,384,4096]{2,1,0:T(8,128)(2,1)} %bitcast.43, bf16[2,4096,768]{2,1,0:T(8,128)(2,1)} %all-gather.6.cloned.1.call-done), kind=kOutput, calls=%fused_computation | convolution fusion | flops 9670361088 | bytes 40108032 | tf_op jit(solution)/shard_map/erf,efd->erd/dot_general | solution.py:49
  490.1 14.7 %reduce-scatter.2.cloned.1.call-done = bf16[2,384,2048]{2,1,0:T(8,128)(2,1)} async-done(((bf16[2,384,4096]{2,1,0:T(8,128)(2,1)}), bf16[2,384,2048]{2,1,0:T(8,128)(2,1)}) %reduce-scatter.2.cloned.1.call-update) | async-done | bytes 3145744 | tf_op jit(solution)/shard_map/reduce_scatter | solution.py:56
  504.7 6.8 %copy.53 = bf16[1,2,384,2048]{3,1,0,2:T(2,128)(2,1)} copy(bf16[1,2,384,2048]{3,2,1,0:T(8,128)(2,1)} %bitcast.44) | data formatting | bytes 6291456 | tf_op jit(solution)/shard_map/broadcast_in_dim | solution.py:62
  511.6 5.6 all-to-all-start.1
  517.1 0.1 copy.51
  517.2 0.5 select_reduce_fusion
  517.8 69.6 %all-to-all-done.1 = bf16[1,2,384,2048]{3,1,0,2:T(2,128)(2,1)S(1)} async-done(((bf16[1,2,384,2048]{3,1,0,2:T(2,128)(2,1)}), bf16[1,2,384,2048]{3,1,0,2:T(2,128)(2,1)S(1)}, u32[]{:S(2)}, u32[]{:S(2)}) %all-to-all-start.1) | async-done | bytes 3145760 | tf_op jit(solution)/shard_map/all_to_all | solution.py:62
  587.3 1.4 copy.54
  588.7 0.4 copy.55
  589.1 0.7 fusion.3
  589.8 1.4 fusion
  (16 shorter events, 0.2 us)
Async XLA Ops:
  6.5 162.0 %all-gather.4.cloned.1.call-start = ((), (), s32[]{:S(2)}) async-start(), calls=%async_computation.3 | async-start | bytes 18874368 | tf_op jit(solution)/shard_map/all_gather | solution.py:39
  7.3 0.8 copy-start.1
  7.3 2.8 copy-start
  7.3 308.1 %all-gather.6.cloned.1.call-start = ((), (), s32[]{:S(2)}) async-start(), calls=%async_computation.4 | async-start | bytes 18874368 | tf_op jit(solution)/shard_map/all_gather | solution.py:45
  17.3 145.0 %all-to-all-start = ((bf16[8,2,48,4096]{3,2,1,0:T(8,128)(2,1)}), bf16[8,2,48,4096]{3,2,1,0:T(8,128)(2,1)}, u32[]{:S(2)}, u32[]{:S(2)}) async-start(bf16[8,2,48,4096]{3,2,1,0:T(8,128)(2,1)} %bitcast.38), calls=%async_computation | async-start | bytes 12582912 | tf_op jit(solution)/shard_map/all_to_all | solution.py:28
  24.6 444.9 %all-gather.8.cloned.1.call-start = ((), (), s32[]{:S(2)}) async-start(), calls=%async_computation.5 | async-start | bytes 18874368 | tf_op jit(solution)/shard_map/all_gather | solution.py:52
  25.3 479.4 %reduce-scatter.2.cloned.1.call-start = ((), (), s32[]{:S(2)}) async-start(), calls=%async_computation.6 | async-start | bytes 9437184 | tf_op jit(solution)/shard_map/reduce_scatter | solution.py:56
  511.6 5.6 copy-start.2
  511.6 75.8 %all-to-all-start.1 = ((bf16[1,2,384,2048]{3,1,0,2:T(2,128)(2,1)}), bf16[1,2,384,2048]{3,1,0,2:T(2,128)(2,1)S(1)}, u32[]{:S(2)}, u32[]{:S(2)}) async-start(bf16[1,2,384,2048]{3,1,0,2:T(2,128)(2,1)} %copy.53), calls=%async_computation.2 | async-start | bytes 6291456 | tf_op jit(solution)/shard_map/all_to_all | solution.py:62
Sparse Core Ops, SparseCore 0:
  8.9 153.4 all-gather.3
  163.9 151.4 all-gather.5
  317.0 152.4 all-gather.7
  490.2 14.4 reduce-scatter.1
where the time goes:
time: 600 us; the launch traced here: 598 us
  waiting for transfers between devices  512 us (85%)
  matrix products  39.5 us (7%)
  local copies, waits for them, and re-layouts  15.7 us (3%)
  between operations  13.2 us (2%)
  starting transfers between devices  13.1 us (2%)
    all_gather x1, waiting for transfers between devices, shards(): lax.all_gather(down_weight, 'dp', axis=2, tiled=True)  154 us
    all_to_all x1, waiting for transfers between devices, shards(): lax.all_to_all(packed.reshape(groups, held_count, capacity, gathered.shap...  137 us
    all_gather x1, waiting for transfers between devices, shards(): lax.all_gather(up_weight, 'dp', axis=1, tiled=True)  134 us
    all_to_all x1, waiting for transfers between devices, shards(): lax.all_to_all(summed[None], 'expert', split_axis=2, concat_axis=0, tiled...  69.6 us
    dot_general x1, matrix products, shards(): jnp.einsum('erf,efd->erd', hidden, lax.all_gather(down_weight, 'dp', axis...  20.5 us
    reduce_scatter x1, waiting for transfers between devices, shards(): lax.psum_scatter(partial_value.astype(jnp.float32).astype(jnp.bfloat16),...  14.7 us
    dot_general x1, matrix products, shards(): jnp.einsum('erd,edf->erf', inputs, lax.all_gather(gate_weight, 'dp', axis...  12.5 us
  transfers between devices with their start and end apart: 6, of which 5 were waited for; matrix products, arithmetic and copies ran while one was open for 4% of the time, Pallas kernels for 0%

commit v1 on v0

v1 whole, which is shorter than its diff:
```python
import jax
import jax.numpy as jnp
from jax import lax
from jax.sharding import PartitionSpec as P


def spread_tokens(tokens, groups, cores, width):
    rows = tokens.shape[0]
    if groups == cores:
        perm = [
            (((d - c) % groups) * cores + d, d * cores + c)
            for d in range(groups)
            for c in range(cores)
        ]
        swapped = lax.ppermute(tokens, ("dp", "etp"), perm)
        along = lax.all_gather(swapped, "expert", axis=0)
        return lax.all_gather(along, "etp", axis=0)
    full = lax.all_gather(tokens, "etp", axis=1, tiled=True)
    mine = lax.all_to_all(
        full.reshape(rows, groups, width), "dp", split_axis=1, concat_axis=0, tiled=False
    )
    mine = mine.reshape(groups, rows, width)
    order = jnp.mod(lax.axis_index("dp") - jnp.arange(groups), groups)
    return lax.all_gather(jnp.take(mine, order, axis=0), "expert", axis=1)


def collect_output(parts, groups, cores, width):
    stacked = jnp.stack(parts)
    if groups == cores:
        summed = lax.psum_scatter(stacked, "etp", scatter_dimension=0, tiled=False)
        summed = lax.psum_scatter(summed, "expert", scatter_dimension=0, tiled=False)
        perm = [
            (d * cores + c, ((d - c) % groups) * cores + d)
            for d in range(groups)
            for c in range(cores)
        ]
        return lax.ppermute(summed, ("dp", "etp"), perm)
    summed = lax.psum_scatter(stacked, "expert", scatter_dimension=1, tiled=False)
    order = jnp.mod(lax.axis_index("dp") - jnp.arange(groups), groups)
    summed = lax.psum(jnp.take(summed, order, axis=0).astype(jnp.float32), "etp")
    back = lax.all_to_all(
        summed.astype(jnp.bfloat16), "dp", split_axis=0, concat_axis=1, tiled=True
    )
    back = back.reshape(back.shape[1] // groups, -1) if back.ndim == 2 else back
    rows = back.shape[-2] // groups
    back = back.reshape(groups, rows, width).transpose(1, 0, 2).reshape(rows, cores, -1)
    return lax.dynamic_index_in_dim(back, lax.axis_index("etp"), 1, keepdims=False)


def shards(tokens, expert_ids, combine, gate_weight, up_weight, down_weight):
    rows, top_count = expert_ids.shape
    held, width, _ = gate_weight.shape
    groups = lax.axis_size("dp")
    columns = lax.axis_size("expert")
    cores = lax.axis_size("etp")
    experts = held * columns
    capacity = min(rows, 3 * rows * top_count // (2 * experts))
    group = lax.axis_index("dp")

    named = expert_ids[:, :, None] == jnp.arange(experts, dtype=jnp.int32)[None, None, :]
    weight = jnp.sum(jnp.where(named, combine[:, :, None], 0.0), axis=1)
    weight = lax.all_gather(weight.T, ("dp", "expert"), axis=0)
    weight = lax.dynamic_slice_in_dim(weight, lax.axis_index("expert") * held, held, axis=1)
    chosen = (weight > 0).astype(jnp.bfloat16)
    earlier = jnp.triu(jnp.ones((rows, rows), jnp.bfloat16), 1)
    place = jnp.einsum("bet,tu->beu", chosen, earlier, preferred_element_type=jnp.float32)
    slots = jnp.arange(capacity, dtype=jnp.float32)[None, None, :, None]
    hit = (place[:, :, None, :] == slots) & (weight > 0)[:, :, None, :]
    picker = hit.astype(jnp.bfloat16).reshape(groups, columns, held, capacity, rows)
    slot_weight = jnp.sum(jnp.where(hit, weight[:, :, None, :], 0.0), axis=-1)
    slot_weight = slot_weight.reshape(groups, columns, held, capacity)

    spread = spread_tokens(tokens, groups, cores, width)

    def pick(r):
        which = jnp.mod(group - r, groups)
        return lax.dynamic_index_in_dim(picker, which, 0, keepdims=False)

    def gate_up(r):
        packed = jnp.einsum(
            "xest,xtk->exsk", pick(r), spread[r], preferred_element_type=jnp.float32
        )
        packed = packed.astype(jnp.bfloat16).reshape(held, columns * capacity, width)
        found = []
        for e in range(held):
            found.append(
                tuple(
                    jnp.dot(packed[e], w[e], preferred_element_type=jnp.float32)
                    for w in (gate_weight, up_weight)
                )
            )
        return found

    gates = [[] for _ in range(held)]
    ups = [[] for _ in range(held)]
    for r in range(1, groups):
        perm = [(d, (d - r) % groups) for d in range(groups)]
        for e, (g, u) in enumerate(gate_up(r)):
            sent = lax.ppermute(
                jnp.concatenate([g, u], axis=1).astype(jnp.bfloat16), "dp", perm
            )
            half = sent.shape[1] // 2
            gates[e].append(sent[:, :half].astype(jnp.float32))
            ups[e].append(sent[:, half:].astype(jnp.float32))
    own_weight = lax.dynamic_index_in_dim(slot_weight, group, 0, keepdims=False)
    own_weight = own_weight.transpose(1, 0, 2).reshape(held, columns * capacity, 1)
    hidden = [[] for _ in range(groups)]
    for e, (g, u) in enumerate(gate_up(0)):
        g = sum(gates[e], g)
        u = sum(ups[e], u)
        h = (jax.nn.silu(g) * u * own_weight[e]).astype(jnp.bfloat16)
        hidden[0].append(h)
        for r in range(1, groups):
            perm = [(d, (d + r) % groups) for d in range(groups)]
            hidden[r].append(lax.ppermute(h, "dp", perm))

    parts = []
    for r in range(groups):
        h = jnp.stack(hidden[r]).reshape(held, columns, capacity, -1)
        dense = jnp.einsum("xest,exsf->xtef", pick(r), h, preferred_element_type=jnp.float32)
        dense = dense.astype(jnp.bfloat16).reshape(columns * rows, -1)
        out = jnp.dot(
            dense, down_weight.reshape(-1, width), preferred_element_type=jnp.float32
        )
        parts.append(out.astype(jnp.bfloat16).reshape(columns, rows, width))
    return collect_output(parts, groups, cores, width)


def solution(mesh):
    placed = (
        P(("dp", "expert"), "etp"),
        P(("dp", "expert"), None),
        P(("dp", "expert"), None),
        P("expert", "dp", "etp"),
        P("expert", "dp", "etp"),
        P("expert", "etp", "dp"),
    )
    return jax.shard_map(
        shards, mesh=mesh, in_specs=placed, out_specs=P(("dp", "expert"), "etp"), check_vma=False
    )
```

time: 600 us -> 293 us (0.49)
  waiting for transfers between devices: 512 us -> 197 us
  blocking collectives: 2.18 us -> 33.2 us
  matrix products: 39.5 us -> 26.1 us
  local copies, waits for them, and re-layouts: 15.7 us -> 7.09 us
    all_gather x3 -> x2, waiting for transfers between devices: 289 us -> 47.4 us  [the longest x1 47.4 us: spread_tokens(): along = lax.all_gather(swapped, 'expert', axis=0)]
    all_to_all x2 -> x0, waiting for transfers between devices: 206 us -> none  [the longest x1 137 us: shards(): lax.all_to_all(packed.reshape(groups, held_count, capacity, gathered.shap...]
    reduce_scatter x1 -> x2, waiting for transfers between devices: 14.7 us -> 88.4 us  [the longest x1 71 us: collect_output(): lax.psum_scatter(summed, 'expert', scatter_dimension=0, tiled=False)]
    ppermute x0 -> x6, waiting for transfers between devices: none -> 61.4 us  [the longest x2 36.2 us: shards(): lax.ppermute(jnp.concatenate([g, u], axis=1).astype(jnp.bfloat16), 'dp',...]
    all_gather x1, blocking collectives: 2.18 us -> 33.2 us  [shards(): weight = lax.all_gather(weight.T, ('dp', 'expert'), axis=0)]
    dot_general x5 -> x15, matrix products: 39.5 us -> 26.1 us  [the longest x8 13.8 us: gate_up(): jnp.dot(packed[e], w[e], preferred_element_type=jnp.float32)]
    all_to_all x2 -> x0, starting transfers between devices: 12.9 us -> none  [the longest x1 7.29 us: shards(): lax.all_to_all(packed.reshape(groups, held_count, capacity, gathered.shap...]
    ppermute x0 -> x6, starting transfers between devices: none -> 11.9 us  [the longest x1 5.18 us: collect_output(): return lax.ppermute(summed, ('dp', 'etp'), perm)]
  transfers between devices with their start and end apart: 6 -> 10, of which waited for: 5 -> 9; matrix products, arithmetic and copies ran while one was open for 4% -> 5% of each run, Pallas kernels for 0% -> 0%
where the time goes in v1:
time: 293 us; the launch traced here: 292 us
  waiting for transfers between devices  197 us (67%)
  blocking collectives  33.2 us (11%)
  matrix products  26.1 us (9%)
  between operations  13.5 us (5%)
  starting transfers between devices  12.1 us (4%)
  local copies, waits for them, and re-layouts  7.09 us (2%)
  other arithmetic  2.99 us (1%)
    reduce_scatter x1, waiting for transfers between devices, collect_output(): lax.psum_scatter(summed, 'expert', scatter_dimension=0, tiled=False)  71 us
    all_gather x1, waiting for transfers between devices, spread_tokens(): along = lax.all_gather(swapped, 'expert', axis=0)  47.4 us
    ppermute x2, waiting for transfers between devices, shards(): lax.ppermute(jnp.concatenate([g, u], axis=1).astype(jnp.bfloat16), 'dp',...  36.2 us
    all_gather x1, blocking collectives, shards(): weight = lax.all_gather(weight.T, ('dp', 'expert'), axis=0)  33.2 us
    reduce_scatter x1, waiting for transfers between devices, collect_output(): summed = lax.psum_scatter(stacked, 'etp', scatter_dimension=0, tiled=False)  17.5 us
    ppermute x2, waiting for transfers between devices, shards(): hidden[r].append(lax.ppermute(h, 'dp', perm))  16.7 us
    dot_general x8, matrix products, gate_up(): jnp.dot(packed[e], w[e], preferred_element_type=jnp.float32)  13.8 us
    dot_general x2, matrix products, shards(): jnp.dot(dense, down_weight.reshape(-1, width), preferred_element_type=jnp...  7.49 us
  transfers between devices with their start and end apart: 10, of which 9 were waited for; matrix products, arithmetic and copies ran while one was open for 5% of the time, Pallas kernels for 0%

profile of v1, /device:TPU:1, one launch (start us, length us, event | category | flops | bytes accessed | tf_op | source)
XLA Modules:
  0.0 292.3 jit_solution(13554512307816280803)
XLA Ops:
  6.5 4.1 %collective-permute-start = (bf16[64,2048]{1,0:T(8,128)(2,1)}, bf16[64,2048]{1,0:T(8,128)(2,1)S(1)}, u32[]{:S(2)}, u32[]{:S(2)}) collective-permute-start(bf16[64,2048]{1,0:T(8,128)(2,1)} %param.6), channel_id=1, source_target_pairs={{0,0},{16,1},{17,16},{1,17},{2,2},{18,3},{19,18},{3,19},{4,4},{20,... | collective-permute-start | bytes 786440 | tf_op jit(solution)/shard_map/ppermute | solution.py:15
  10.6 4.8 %collective-permute-done = bf16[64,2048]{1,0:T(8,128)(2,1)S(1)} collective-permute-done((bf16[64,2048]{1,0:T(8,128)(2,1)}, bf16[64,2048]{1,0:T(8,128)(2,1)S(1)}, u32[]{:S(2)}, u32[]{:S(2)}) %collective-permute-start) | collective-permute-done | bytes 262176 | tf_op jit(solution)/shard_map/ppermute | solution.py:15
  15.4 0.7 copy-done.1
  16.2 47.4 %all-gather.6.cloned.1.call-done = bf16[512,2048]{1,0:T(8,128)(2,1)} async-done(((bf16[64,2048]{1,0:T(8,128)(2,1)}), bf16[512,2048]{1,0:T(8,128)(2,1)}) %all-gather.6.cloned.1.call-update) | async-done | bytes 2097168 | tf_op jit(solution)/shard_map/all_gather | solution.py:16
  63.7 33.2 %all-gather = f32[256,64]{1,0:T(8,128)S(1)} all-gather(f32[16,64]{1,0:T(8,128)S(1)} %bitcast.137), channel_id=2, replica_groups=mesh['dp'=2,'expert'=8,'etp'=2] {'dp','expert'}, dimensions={0}, use_global_device_ids=true | all-gather | bytes 69632 | tf_op jit(solution)/shard_map/all_gather | solution.py:62
  98.0 2.6 fusion.17
  101.0 3.5 %fusion.37 = bf16[384,768]{1,0:T(8,128)(2,1)S(1)} fusion(bf16[384,2048]{1,0:T(8,128)(2,1)S(1)} %bitcast.128, bf16[2,2048,768]{2,1,0:T(8,128)(2,1)} %param.10), kind=kOutput, calls=%fused_computation.40 | convolution fusion | flops 1208254464 | bytes 5308416 | tf_op jit(solution)/shard_map/dot_general | solution.py:88
  104.5 1.4 fusion.34
  106.4 1.4 fusion.31
  107.7 1.4 fusion.28
  109.8 1.2 collective-permute-start.2
  111.3 1.0 fusion.16
  112.7 1.4 fusion.6
  114.1 1.4 fusion.14
  115.5 13.1 %collective-permute-done.1 = bf16[384,1536]{1,0:T(8,128)(2,1)S(1)} collective-permute-done((bf16[384,1536]{1,0:T(8,128)(2,1)S(1)}, bf16[384,1536]{1,0:T(8,128)(2,1)S(1)}, u32[]{:S(2)}, u32[]{:S(2)}) %collective-permute-start.1) | collective-permute-done | bytes 1179680 | tf_op jit(solution)/shard_map/ppermute | solution.py:99
  128.6 1.6 multiply_convert_fusion.1
  130.7 23.2 %collective-permute-done.2 = bf16[384,1536]{1,0:T(8,128)(2,1)S(1)} collective-permute-done((bf16[384,1536]{1,0:T(8,128)(2,1)S(1)}, bf16[384,1536]{1,0:T(8,128)(2,1)S(1)}, u32[]{:S(2)}, u32[]{:S(2)}) %collective-permute-start.2) | collective-permute-done | bytes 1179680 | tf_op jit(solution)/shard_map/ppermute | solution.py:99
  153.9 1.8 multiply_convert_fusion
  156.2 0.6 fusion.26
  156.8 1.6 copy.54
  158.7 3.7 %convolution_convert_fusion.3 = bf16[512,2048]{1,0:T(8,128)(2,1)S(1)} fusion(bf16[512,1536]{1,0:T(8,128)(2,1)S(1)} %bitcast.120, bf16[1536,2048]{1,0:T(8,128)(2,1)S(1)} %bitcast.144), kind=kOutput, calls=%fused_computation.22 | convolution fusion | flops 3222274048 | bytes 9961472 | tf_op jit(solution)/shard_map/dot_general | solution.py:122
  162.5 4.0 %collective-permute-done.3 = bf16[384,768]{1,0:T(8,128)(2,1)S(1)} collective-permute-done((bf16[384,768]{1,0:T(8,128)(2,1)S(1)}, bf16[384,768]{1,0:T(8,128)(2,1)S(1)}, u32[]{:S(2)}, u32[]{:S(2)}) %collective-permute-start.3) | collective-permute-done | bytes 589856 | tf_op jit(solution)/shard_map/ppermute | solution.py:115
  166.5 12.6 %collective-permute-done.4 = bf16[384,768]{1,0:T(8,128)(2,1)S(1)} collective-permute-done((bf16[384,768]{1,0:T(8,128)(2,1)S(1)}, bf16[384,768]{1,0:T(8,128)(2,1)S(1)}, u32[]{:S(2)}, u32[]{:S(2)}) %collective-permute-start.4) | collective-permute-done | bytes 589856 | tf_op jit(solution)/shard_map/ppermute | solution.py:115
  179.1 0.6 fusion.27
  179.8 1.6 copy.57
  181.7 3.7 %convolution_convert_fusion.2 = bf16[512,2048]{1,0:T(8,128)(2,1)S(1)} fusion(bf16[512,1536]{1,0:T(8,128)(2,1)S(1)} %bitcast.121, bf16[1536,2048]{1,0:T(8,128)(2,1)S(1)} %bitcast.145), kind=kOutput, calls=%fused_computation.21 | convolution fusion | flops 3222274048 | bytes 9961472 | tf_op jit(solution)/shard_map/dot_general | solution.py:122
  185.4 2.3 pad_maximum_fusion
  187.8 17.5 %reduce-scatter.3.cloned.1.call-done = bf16[1,8,64,2048]{3,2,1,0:T(8,128)(2,1)} async-done(((bf16[2,8,64,2048]{3,2,1,0:T(8,128)(2,1)}), bf16[1,8,64,2048]{3,2,1,0:T(8,128)(2,1)}) %reduce-scatter.3.cloned.1.call-update) | async-done | bytes 2097168 | tf_op jit(solution)/shard_map/reduce_scatter | solution.py:30
  205.3 71.0 %reduce-scatter.5.cloned.1.call-done = bf16[1,64,2048]{2,1,0:T(8,128)(2,1)} async-done(((bf16[8,64,2048]{2,1,0:T(8,128)(2,1)}), bf16[1,64,2048]{2,1,0:T(8,128)(2,1)}) %reduce-scatter.5.cloned.1.call-update) | async-done | bytes 262160 | tf_op jit(solution)/shard_map/reduce_scatter | solution.py:31
  276.3 5.2 %collective-permute-start.5 = (bf16[64,2048]{1,0:T(8,128)(2,1)}, bf16[64,2048]{1,0:T(8,128)(2,1)S(1)}, u32[]{:S(2)}, u32[]{:S(2)}) collective-permute-start(bf16[64,2048]{1,0:T(8,128)(2,1)} %bitcast.146), channel_id=1, source_target_pairs={{0,0},{1,16},{16,17},{17,1},{2,2},{3,18},{18,19},{19,3},{4,4},{5,2... | collective-permute-start | bytes 786440 | tf_op jit(solution)/shard_map/ppermute | solution.py:37
  281.4 3.6 %collective-permute-done.5 = bf16[64,2048]{1,0:T(8,128)(2,1)S(1)} collective-permute-done((bf16[64,2048]{1,0:T(8,128)(2,1)}, bf16[64,2048]{1,0:T(8,128)(2,1)S(1)}, u32[]{:S(2)}, u32[]{:S(2)}) %collective-permute-start.5) | collective-permute-done | bytes 262176 | tf_op jit(solution)/shard_map/ppermute | solution.py:37
  285.1 0.7 copy.67
  (55 shorter events, 5.0 us)
Async XLA Ops:
  6.5 57.2 %copy-start.2 = (f32[64,8]{0,1:T(8,128)S(1)}, f32[64,8]{0,1:T(8,128)}, u32[]{:S(2)}) copy-start(f32[64,8]{0,1:T(8,128)} %param.8) | copy-start | bytes 6148
  6.5 57.2 %copy-start.3 = (s32[64,8]{0,1:T(8,128)S(1)}, s32[64,8]{0,1:T(8,128)}, u32[]{:S(2)}) copy-start(s32[64,8]{0,1:T(8,128)} %param.7) | copy-start | bytes 6148
  6.5 57.0 %all-gather.6.cloned.1.call-start = ((), (), s32[]{:S(2)}) async-start(), calls=%async_computation.4 | async-start | bytes 2359296 | tf_op jit(solution)/shard_map/all_gather | solution.py:16
  6.5 8.9 %collective-permute-start = (bf16[64,2048]{1,0:T(8,128)(2,1)}, bf16[64,2048]{1,0:T(8,128)(2,1)S(1)}, u32[]{:S(2)}, u32[]{:S(2)}) collective-permute-start(bf16[64,2048]{1,0:T(8,128)(2,1)} %param.6), channel_id=1, source_target_pairs={{0,0},{16,1},{17,16},{1,17},{2,2},{18,3},{19,18},{3,19},{4,4},{20,... | collective-permute-start | bytes 786440 | tf_op jit(solution)/shard_map/ppermute | solution.py:15
  15.4 0.7 copy-start.1
  16.2 81.8 %all-gather.8.cloned.1.call-start = ((), (), s32[]{:S(2)}) async-start(), calls=%async_computation.5 | async-start | bytes 6291456 | tf_op jit(solution)/shard_map/all_gather | solution.py:17
  63.6 141.7 %reduce-scatter.3.cloned.1.call-start = ((), (), s32[]{:S(2)}) async-start(), calls=%async_computation.2 | async-start | bytes 6291456 | tf_op jit(solution)/shard_map/reduce_scatter | solution.py:30
  100.5 4.0 %slice-start = ((s8[6291456]{0:T(1024)(128)(4,1)}), s8[4194304]{0:T(1024)(128)(4,1)S(1)}, s32[]{:S(2)}) async-start(s8[6291456]{0:T(1024)(128)(4,1)} %bitcast.138), calls=%async_computation.6 | async-start | bytes 8388608
  100.9 3.6 %slice-start.1 = ((s8[6291456]{0:T(1024)(128)(4,1)}), s8[2097152]{0:T(1024)(128)(4,1)S(1)}, s32[]{:S(2)}) async-start(s8[6291456]{0:T(1024)(128)(4,1)} %bitcast.138), calls=%async_computation.7 | async-start | bytes 4194304
  100.9 5.0 %slice-start.2 = ((s8[6291456]{0:T(1024)(128)(4,1)}), s8[4194304]{0:T(1024)(128)(4,1)S(1)}, s32[]{:S(2)}) async-start(s8[6291456]{0:T(1024)(128)(4,1)} %bitcast.140), calls=%async_computation.8 | async-start | bytes 8388608
  104.5 1.8 slice-start.3
  109.1 2.2 copy-start
  109.2 19.3 %collective-permute-start.1 = (bf16[384,1536]{1,0:T(8,128)(2,1)S(1)}, bf16[384,1536]{1,0:T(8,128)(2,1)S(1)}, u32[]{:S(2)}, u32[]{:S(2)}) collective-permute-start(bf16[384,1536]{1,0:T(8,128)(2,1)S(1)} %pad_maximum_fusion.1), channel_id=1, source_target_pairs={{0,16},{16,0},{1,17},{17,1},{2,18},{18,2},{3,19},{19,3},{4,20},{20... | collective-permute-start | bytes 3538952 | tf_op jit(solution)/shard_map/ppermute | solution.py:99
  109.8 44.1 %collective-permute-start.2 = (bf16[384,1536]{1,0:T(8,128)(2,1)S(1)}, bf16[384,1536]{1,0:T(8,128)(2,1)S(1)}, u32[]{:S(2)}, u32[]{:S(2)}) collective-permute-start(bf16[384,1536]{1,0:T(8,128)(2,1)S(1)} %pad_maximum_fusion.2), channel_id=1, source_target_pairs={{0,16},{16,0},{1,17},{17,1},{2,18},{18,2},{3,19},{19,3},{4,20},{20... | collective-permute-start | bytes 3538952 | tf_op jit(solution)/shard_map/ppermute | solution.py:99
  128.6 30.1 %slice-start.4 = ((s8[6291456]{0:T(1024)(128)(4,1)}), s8[4194304]{0:T(1024)(128)(4,1)S(1)}, s32[]{:S(2)}) async-start(s8[6291456]{0:T(1024)(128)(4,1)} %bitcast.142), calls=%async_computation.10 | async-start | bytes 8388608
  130.2 28.5 %slice-start.5 = ((s8[6291456]{0:T(1024)(128)(4,1)}), s8[2097152]{0:T(1024)(128)(4,1)S(1)}, s32[]{:S(2)}) async-start(s8[6291456]{0:T(1024)(128)(4,1)} %bitcast.142), calls=%async_computation.11 | async-start | bytes 4194304
  130.2 36.3 %collective-permute-start.3 = (bf16[384,768]{1,0:T(8,128)(2,1)S(1)}, bf16[384,768]{1,0:T(8,128)(2,1)S(1)}, u32[]{:S(2)}, u32[]{:S(2)}) collective-permute-start(bf16[384,768]{1,0:T(8,128)(2,1)S(1)} %multiply_convert_fusion.1), channel_id=1, source_target_pairs={{0,16},{16,0},{1,17},{17,1},{2,18},{18,2},{3,19},{19,3},{4,20},{20... | collective-permute-start | bytes 1769480 | tf_op jit(solution)/shard_map/ppermute | solution.py:115
  155.6 23.5 %collective-permute-start.4 = (bf16[384,768]{1,0:T(8,128)(2,1)S(1)}, bf16[384,768]{1,0:T(8,128)(2,1)S(1)}, u32[]{:S(2)}, u32[]{:S(2)}) collective-permute-start(bf16[384,768]{1,0:T(8,128)(2,1)S(1)} %multiply_convert_fusion), channel_id=1, source_target_pairs={{0,16},{16,0},{1,17},{17,1},{2,18},{18,2},{3,19},{19,3},{4,20},{20... | collective-permute-start | bytes 1769480 | tf_op jit(solution)/shard_map/ppermute | solution.py:115
  187.7 88.5 %reduce-scatter.5.cloned.1.call-start = ((), (), s32[]{:S(2)}) async-start(), calls=%async_computation.3 | async-start | bytes 2359296 | tf_op jit(solution)/shard_map/reduce_scatter | solution.py:31
  276.3 8.8 %collective-permute-start.5 = (bf16[64,2048]{1,0:T(8,128)(2,1)}, bf16[64,2048]{1,0:T(8,128)(2,1)S(1)}, u32[]{:S(2)}, u32[]{:S(2)}) collective-permute-start(bf16[64,2048]{1,0:T(8,128)(2,1)} %bitcast.146), channel_id=1, source_target_pairs={{0,0},{1,16},{16,17},{17,1},{2,2},{3,18},{18,19},{19,3},{4,4},{5,2... | collective-permute-start | bytes 786440 | tf_op jit(solution)/shard_map/ppermute | solution.py:37
Sparse Core Ops, SparseCore 0:
  16.3 47.2 all-gather.5
  65.1 14.4 all-gather.7
  187.9 17.3 reduce-scatter.2
  208.6 67.5 reduce-scatter.4

commit v2 on v1

--- a/solution.py
+++ b/solution.py
@@ -2,6 +2,65 @@
 import jax.numpy as jnp
 from jax import lax
 from jax.sharding import PartitionSpec as P
+
+
+def ring_steps(columns):
+    ring = list(range(0, columns, 2)) + list(range(1, columns, 2))[::-1]
+    ahead = [(ring[i], ring[(i + 1) % columns]) for i in range(columns)]
+    return ahead, [(b, a) for a, b in ahead]
+
+
+def ring_spread(block, groups, columns, cores):
+    perm = [
+        (((d - c) % groups) * cores + d, d * cores + c) for d in range(groups) for c in range(cores)
+    ]
+    ahead, back = ring_steps(columns)
+    block = lax.ppermute(block, ("dp", "etp"), perm)
+    held = {0: block}
+    up = down = block
+    for step in range(1, columns // 2 + 1):
+        up = lax.ppermute(up, "expert", ahead)
+        held[step] = up
+        if columns - step > step:
+            down = lax.ppermute(down, "expert", back)
+            held[columns - step] = down
+    swap = [(0, 1), (1, 0)]
+    other = {k: lax.ppermute(held[k], "etp", swap) for k in held}
+    first = lax.axis_index("etp") == 0
+    pairs = [(held[k], other[k]) for k in range(columns)]
+    return (
+        jnp.stack([jnp.where(first, a, b) for a, b in pairs]),
+        jnp.stack([jnp.where(first, b, a) for a, b in pairs]),
+    )
+
+
+def ring_collect(parts, groups, columns, cores):
+    ahead, back = ring_steps(columns)
+    first = lax.axis_index("etp") == 0
+    mine = jnp.where(first, parts[0], parts[1])
+    away = jnp.where(first, parts[1], parts[0])
+    half = mine.shape[1] // 2
+    order = [k for s in range(1, columns // 2 + 1) for k in (s, columns - s)] + [0]
+    other = {}
+    for k in order:
+        if k not in other:
+            other[k] = lax.ppermute(away[k], "etp", [(0, 1), (1, 0)])
+
+    def own(k, low):
+        rows = slice(0, half) if low else slice(half, None)
+        return mine[k, rows].astype(jnp.float32) + other[k][rows].astype(jnp.float32)
+
+    up = own(1, True).astype(jnp.bfloat16)
+    down = own(columns - 1, False).astype(jnp.bfloat16)
+    for step in range(2, columns + 1):
+        up = lax.ppermute(up, "expert", ahead)
+        down = lax.ppermute(down, "expert", back)
+        up = (up.astype(jnp.float32) + own(step % columns, True)).astype(jnp.bfloat16)
+        down = (down.astype(jnp.float32) + own(columns - step, False)).astype(jnp.bfloat16)
+    perm = [
+        (d * cores + c, ((d - c) % groups) * cores + d) for d in range(groups) for c in range(cores)
+    ]
+    return lax.ppermute(jnp.concatenate([up, down]), ("dp", "etp"), perm)
 
 
 def spread_tokens(tokens, groups, cores, width):
@@ -59,7 +118,22 @@
 
     named = expert_ids[:, :, None] == jnp.arange(experts, dtype=jnp.int32)[None, None, :]
     weight = jnp.sum(jnp.where(named, combine[:, :, None], 0.0), axis=1)
-    weight = lax.all_gather(weight.T, ("dp", "expert"), axis=0)
+    near = groups == cores == 2 and columns % 2 == 0
+    if near:
+        high = weight.T.astype(jnp.bfloat16)
+        low = (weight.T - high.astype(jnp.float32)).astype(jnp.bfloat16)
+        extra = jnp.stack([high, low]).reshape(-1)
+        extra_rows = -(-extra.size // (8 * tokens.shape[1])) * 8
+        extra = jnp.pad(extra, (0, extra_rows * tokens.shape[1] - extra.size))
+        block = jnp.concatenate([tokens, extra.reshape(extra_rows, -1)])
+        whole = ring_spread(block, groups, columns, cores)
+        spread = [a[:, :rows] for a in whole]
+        tail = jnp.stack([a[:, rows:] for a in whole]).reshape(groups * columns, -1)
+        tail = tail[:, : 2 * experts * rows].reshape(-1, 2, experts, rows).astype(jnp.float32)
+        weight = tail[:, 0] + tail[:, 1]
+    else:
+        spread = spread_tokens(tokens, groups, cores, width)
+        weight = lax.all_gather(weight.T, ("dp", "expert"), axis=0)
     weight = lax.dynamic_slice_in_dim(weight, lax.axis_index("expert") * held, held, axis=1)
     chosen = (weight > 0).astype(jnp.bfloat16)
     earlier = jnp.triu(jnp.ones((rows, rows), jnp.bfloat16), 1)
@@ -70,10 +144,8 @@
     slot_weight = jnp.sum(jnp.where(hit, weight[:, :, None, :], 0.0), axis=-1)
     slot_weight = slot_weight.reshape(groups, columns, held, capacity)
 
-    spread = spread_tokens(tokens, groups, cores, width)
-
     def pick(r):
-        which = jnp.mod(group - r, groups)
+        which = r if near else jnp.mod(group - r, groups)
         return lax.dynamic_index_in_dim(picker, which, 0, keepdims=False)
 
     def gate_up(r):
@@ -102,7 +174,7 @@
             half = sent.shape[1] // 2
             gates[e].append(sent[:, :half].astype(jnp.float32))
             ups[e].append(sent[:, half:].astype(jnp.float32))
-    own_weight = lax.dynamic_index_in_dim(slot_weight, group, 0, keepdims=False)
+    own_weight = lax.dynamic_index_in_dim(slot_weight, 0 if near else group, 0, keepdims=False)
     own_weight = own_weight.transpose(1, 0, 2).reshape(held, columns * capacity, 1)
     hidden = [[] for _ in range(groups)]
     for e, (g, u) in enumerate(gate_up(0)):
@@ -123,6 +195,8 @@
             dense, down_weight.reshape(-1, width), preferred_element_type=jnp.float32
         )
         parts.append(out.astype(jnp.bfloat16).reshape(columns, rows, width))
+    if near:
+        return ring_collect(parts, groups, columns, cores)
     return collect_output(parts, groups, cores, width)
 
 

time: 293 us -> 232 us (0.79)
  waiting for transfers between devices: 197 us -> 115 us
  starting transfers between devices: 12.1 us -> 71.7 us
  blocking collectives: 33.2 us -> 0 us
  between operations: 13.5 us -> 0.59 us
  other arithmetic: 2.99 us -> 6.2 us
    reduce_scatter x2 -> x0, waiting for transfers between devices: 88.4 us -> none  [the longest x1 71 us: collect_output(): lax.psum_scatter(summed, 'expert', scatter_dimension=0, tiled=False)]
    ppermute x2 -> x39, starting transfers between devices: 9.26 us -> 65.5 us  [the longest x8 25 us: ring_collect(): other[k] = lax.ppermute(away[k], 'etp', [(0, 1), (1, 0)])]
    ppermute x2 -> x39, waiting for transfers between devices: 8.42 us -> 57.5 us  [the longest x4 22.8 us: ring_spread(): up = lax.ppermute(up, 'expert', ahead)]
    all_gather x2 -> x0, waiting for transfers between devices: 47.4 us -> none  [the longest x1 47.4 us: spread_tokens(): along = lax.all_gather(swapped, 'expert', axis=0)]
    all_gather x1 -> x0, blocking collectives: 33.2 us -> none  [shards(): weight = lax.all_gather(weight.T, ('dp', 'expert'), axis=0)]
    dot_general x8, matrix products: 13.8 us -> 18.3 us  [gate_up(): jnp.dot(packed[e], w[e], preferred_element_type=jnp.float32)]
  transfers between devices with their start and end apart: 10 -> 43, of which waited for: 9 -> 21; matrix products, arithmetic and copies ran while one was open for 5% -> 8% of each run, Pallas kernels for 0% -> 0%
where the time goes in v2:
time: 232 us; the launch traced here: 231 us
  waiting for transfers between devices  115 us (50%)
  starting transfers between devices  71.7 us (31%)
  matrix products  28.9 us (12%)
  local copies, waits for them, and re-layouts  9.42 us (4%)
  other arithmetic  6.2 us (3%)
    ppermute x2, waiting for transfers between devices, shards(): lax.ppermute(jnp.concatenate([g, u], axis=1).astype(jnp.bfloat16), 'dp',...  38.5 us
    ppermute x8, starting transfers between devices, ring_collect(): other[k] = lax.ppermute(away[k], 'etp', [(0, 1), (1, 0)])  25 us
    ppermute x4, waiting for transfers between devices, ring_spread(): up = lax.ppermute(up, 'expert', ahead)  22.8 us
    ppermute x2, waiting for transfers between devices, shards(): hidden[r].append(lax.ppermute(h, 'dp', perm))  18.5 us
    dot_general x8, matrix products, gate_up(): jnp.dot(packed[e], w[e], preferred_element_type=jnp.float32)  18.3 us
    ppermute x7, waiting for transfers between devices, ring_collect(): down = lax.ppermute(down, 'expert', back)  13.1 us
    ppermute x7, starting transfers between devices, ring_collect(): down = lax.ppermute(down, 'expert', back)  12 us
    ppermute x7, waiting for transfers between devices, ring_collect(): up = lax.ppermute(up, 'expert', ahead)  10.8 us
  transfers between devices with their start and end apart: 43, of which 21 were waited for; matrix products, arithmetic and copies ran while one was open for 8% of the time, Pallas kernels for 0%

profile of v2, /device:TPU:1, one launch (start us, length us, event | category | flops | bytes accessed | tf_op | source)
XLA Modules:
  0.0 231.4 jit_solution(8014396012982907440)
XLA Ops:
  1.9 4.0 %collective-permute-start = (bf16[72,2048]{1,0:T(8,128)(2,1)S(1)}, bf16[72,2048]{1,0:T(8,128)(2,1)S(1)}, u32[]{:S(2)}, u32[]{:S(2)}) collective-permute-start(bf16[72,2048]{1,0:T(8,128)(2,1)S(1)} %pad_maximum_fusion.2), channel_id=1, source_target_pairs={{0,0},{16,1},{17,16},{1,17},{2,2},{18,3},{19,18},{3,19},{4,4},{20,... | collective-permute-start | bytes 884744 | tf_op jit(solution)/shard_map/ppermute | solution.py:18
  5.8 5.2 %collective-permute-done = bf16[72,2048]{1,0:T(8,128)(2,1)S(1)} collective-permute-done((bf16[72,2048]{1,0:T(8,128)(2,1)S(1)}, bf16[72,2048]{1,0:T(8,128)(2,1)S(1)}, u32[]{:S(2)}, u32[]{:S(2)}) %collective-permute-start) | collective-permute-done | bytes 294944 | tf_op jit(solution)/shard_map/ppermute | solution.py:18
  12.5 4.1 %collective-permute-done.2 = bf16[72,2048]{1,0:T(8,128)(2,1)S(1)} collective-permute-done((bf16[72,2048]{1,0:T(8,128)(2,1)S(1)}, bf16[72,2048]{1,0:T(8,128)(2,1)S(1)}, u32[]{:S(2)}, u32[]{:S(2)}) %collective-permute-start.2) | collective-permute-done | bytes 294944 | tf_op jit(solution)/shard_map/ppermute | solution.py:22
  19.3 5.4 %collective-permute-done.4 = bf16[72,2048]{1,0:T(8,128)(2,1)S(1)} collective-permute-done((bf16[72,2048]{1,0:T(8,128)(2,1)S(1)}, bf16[72,2048]{1,0:T(8,128)(2,1)S(1)}, u32[]{:S(2)}, u32[]{:S(2)}) %collective-permute-start.4) | collective-permute-done | bytes 294944 | tf_op jit(solution)/shard_map/ppermute | solution.py:22
  28.2 6.4 %collective-permute-done.6 = bf16[72,2048]{1,0:T(8,128)(2,1)S(1)} collective-permute-done((bf16[72,2048]{1,0:T(8,128)(2,1)S(1)}, bf16[72,2048]{1,0:T(8,128)(2,1)S(1)}, u32[]{:S(2)}, u32[]{:S(2)}) %collective-permute-start.6) | collective-permute-done | bytes 294944 | tf_op jit(solution)/shard_map/ppermute | solution.py:22
  37.2 6.9 %collective-permute-done.8 = bf16[72,2048]{1,0:T(8,128)(2,1)S(1)} collective-permute-done((bf16[72,2048]{1,0:T(8,128)(2,1)S(1)}, bf16[72,2048]{1,0:T(8,128)(2,1)S(1)}, u32[]{:S(2)}, u32[]{:S(2)}) %collective-permute-start.8) | collective-permute-done | bytes 294944 | tf_op jit(solution)/shard_map/ppermute | solution.py:22
  60.0 3.8 %collective-permute-start.16 = (bf16[384,1536]{1,0:T(8,128)(2,1)}, bf16[384,1536]{1,0:T(8,128)(2,1)}, u32[]{:S(2)}, u32[]{:S(2)}) collective-permute-start(bf16[384,1536]{1,0:T(8,128)(2,1)} %pad_maximum_fusion), channel_id=1, source_target_pairs={{0,16},{16,0},{1,17},{17,1},{2,18},{18,2},{3,19},{19,3},{4,20},{20... | collective-permute-start | bytes 3538952 | tf_op jit(solution)/shard_map/ppermute | solution.py:171
  65.5 2.5 %fusion.14 = f32[384,768]{1,0:T(8,128)} fusion(bf16[384,2048]{1,0:T(8,128)(2,1)S(1)} %bitcast.265, bf16[2,2048,768]{2,1,0:T(8,128)(2,1)S(1)} %bitcast.275), kind=kOutput, calls=%fused_computation.16 | convolution fusion | flops 1207959552 | bytes 5898240 | tf_op jit(solution)/shard_map/dot_general | solution.py:160
  68.2 3.4 %fusion.6 = f32[384,768]{1,0:T(8,128)S(1)} fusion(bf16[384,2048]{1,0:T(8,128)(2,1)S(1)} %bitcast.263, bf16[2,2048,768]{2,1,0:T(8,128)(2,1)} %param.9), kind=kOutput, calls=%fused_computation.8 | convolution fusion | flops 1207959552 | bytes 5898240 | tf_op jit(solution)/shard_map/dot_general | solution.py:160
  71.7 18.4 %collective-permute-done.16 = bf16[384,1536]{1,0:T(8,128)(2,1)} collective-permute-done((bf16[384,1536]{1,0:T(8,128)(2,1)}, bf16[384,1536]{1,0:T(8,128)(2,1)}, u32[]{:S(2)}, u32[]{:S(2)}) %collective-permute-start.16) | collective-permute-done | bytes 1179680 | tf_op jit(solution)/shard_map/ppermute | solution.py:171
  90.1 3.9 %multiply_convert_fusion.1 = bf16[384,768]{1,0:T(8,128)(2,1)S(1)} fusion(f32[384,768]{1,0:T(8,128)S(1)} %copy-done.2, bf16[384,1536]{1,0:T(8,128)(2,1)} %collective-permute-done.16, f32[384]{0:T(512)S(1)} %mul.39, bf16[384,2048]{1,0:T(8,128)(2,1)S(1)} %bitcast.266, bf16[2,2048,768]{2,1,0:T(8,128)(2,1)} %param.10), kind=kOutput, calls=%fused_computation.51 | convolution fusion | flops 1211203584 | bytes 7669248 | tf_op jit(solution)/shard_map/dot_general | solution.py:160
  95.3 20.1 %collective-permute-done.17 = bf16[384,1536]{1,0:T(8,128)(2,1)} collective-permute-done((bf16[384,1536]{1,0:T(8,128)(2,1)}, bf16[384,1536]{1,0:T(8,128)(2,1)}, u32[]{:S(2)}, u32[]{:S(2)}) %collective-permute-start.17) | collective-permute-done | bytes 1179680 | tf_op jit(solution)/shard_map/ppermute | solution.py:171
  115.4 2.8 %multiply_convert_fusion = bf16[384,768]{1,0:T(8,128)(2,1)S(1)} fusion(f32[384,768]{1,0:T(8,128)S(1)} %fusion.6, bf16[384,1536]{1,0:T(8,128)(2,1)} %collective-permute-done.17, f32[384]{0:T(512)S(1)} %mul.44, bf16[384,2048]{1,0:T(8,128)(2,1)S(1)} %bitcast.264, bf16[2,2048,768]{2,1,0:T(8,128)(2,1)S(1)} %bitcast.279), kind=kOutput, calls=%fused_computation.50 | convolution fusion | flops 1211203584 | bytes 7669760 | tf_op jit(solution)/shard_map/dot_general | solution.py:160
  122.0 5.9 %collective-permute-done.18 = bf16[384,768]{1,0:T(8,128)(2,1)S(1)} collective-permute-done((bf16[384,768]{1,0:T(8,128)(2,1)S(1)}, bf16[384,768]{1,0:T(8,128)(2,1)S(1)}, u32[]{:S(2)}, u32[]{:S(2)}) %collective-permute-start.18) | collective-permute-done | bytes 589856 | tf_op jit(solution)/shard_map/ppermute | solution.py:187
  127.9 12.6 %collective-permute-done.19 = bf16[384,768]{1,0:T(8,128)(2,1)S(1)} collective-permute-done((bf16[384,768]{1,0:T(8,128)(2,1)S(1)}, bf16[384,768]{1,0:T(8,128)(2,1)S(1)}, u32[]{:S(2)}, u32[]{:S(2)}) %collective-permute-start.19) | collective-permute-done | bytes 589856 | tf_op jit(solution)/shard_map/ppermute | solution.py:187
  143.1 3.7 %convolution_convert_fusion.2 = bf16[512,2048]{1,0:T(8,128)(2,1)S(1)} fusion(bf16[512,1536]{1,0:T(8,128)(2,1)S(1)} %bitcast.262, bf16[1536,2048]{1,0:T(8,128)(2,1)S(1)} %bitcast.282), kind=kOutput, calls=%fused_computation.20 | convolution fusion | flops 3222274048 | bytes 9961472 | tf_op jit(solution)/shard_map/dot_general | solution.py:194
  146.8 3.6 %broadcast_select_fusion.1 = (bf16[512,2048]{1,0:T(8,128)(2,1)S(1)}, bf16[512,2048]{1,0:T(8,128)(2,1)S(1)}) fusion(bf16[512,2048]{1,0:T(8,128)(2,1)S(1)} %convolution_convert_fusion.2, pred[]{:T(512)S(6)} %eq.39, bf16[512,1536]{1,0:T(8,128)(2,1)S(1)} %bitcast.261, bf16[1536,2048]{1,0:T(8,128)(2,1)S(1)} %bitcast.283), kind=kOutput, calls=%fused_computation.33 | convolution fusion | flops 3224371200 | bytes 14155777 | tf_op jit(solution)/shard_map/dot_general | solution.py:194
  155.0 2.7 %collective-permute-done.21 = bf16[32,2048]{1,0:T(8,128)(2,1)S(1)} collective-permute-done((bf16[32,2048]{1,0:T(8,128)(2,1)S(1)}, bf16[32,2048]{1,0:T(8,128)(2,1)S(1)}, u32[]{:S(2)}, u32[]{:S(2)}) %collective-permute-start.21) | collective-permute-done | bytes 131104 | tf_op jit(solution)/shard_map/ppermute | solution.py:56
  163.0 2.7 %collective-permute-start.28 = (bf16[64,2048]{1,0:T(8,128)(2,1)S(1)}, bf16[64,2048]{1,0:T(8,128)(2,1)S(1)}, u32[]{:S(2)}, u32[]{:S(2)}) collective-permute-start(bf16[64,2048]{1,0:T(8,128)(2,1)S(1)} %get-tuple-element.20), channel_id=1, source_target_pairs={{0,1},{1,0},{2,3},{3,2},{4,5},{5,4},{6,7},{7,6},{8,9},{9,8},{10,11... | collective-permute-start | bytes 786440 | tf_op jit(solution)/shard_map/ppermute | solution.py:47
  167.1 3.9 %collective-permute-start.30 = (bf16[64,2048]{1,0:T(8,128)(2,1)S(1)}, bf16[64,2048]{1,0:T(8,128)(2,1)S(1)}, u32[]{:S(2)}, u32[]{:S(2)}) collective-permute-start(bf16[64,2048]{1,0:T(8,128)(2,1)S(1)} %get-tuple-element.19), channel_id=1, source_target_pairs={{0,1},{1,0},{2,3},{3,2},{4,5},{5,4},{6,7},{7,6},{8,9},{9,8},{10,11... | collective-permute-start | bytes 786440 | tf_op jit(solution)/shard_map/ppermute | solution.py:47
  172.3 3.9 %collective-permute-start.32 = (bf16[64,2048]{1,0:T(8,128)(2,1)S(1)}, bf16[64,2048]{1,0:T(8,128)(2,1)S(1)}, u32[]{:S(2)}, u32[]{:S(2)}) collective-permute-start(bf16[64,2048]{1,0:T(8,128)(2,1)S(1)} %get-tuple-element.18), channel_id=1, source_target_pairs={{0,1},{1,0},{2,3},{3,2},{4,5},{5,4},{6,7},{7,6},{8,9},{9,8},{10,11... | collective-permute-start | bytes 786440 | tf_op jit(solution)/shard_map/ppermute | solution.py:47
  177.5 3.6 %collective-permute-done.31 = bf16[32,2048]{1,0:T(8,128)(2,1)S(1)} collective-permute-done((bf16[32,2048]{1,0:T(8,128)(2,1)S(1)}, bf16[32,2048]{1,0:T(8,128)(2,1)S(1)}, u32[]{:S(2)}, u32[]{:S(2)}) %collective-permute-start.31) | collective-permute-done | bytes 131104 | tf_op jit(solution)/shard_map/ppermute | solution.py:56
  181.2 2.0 collective-permute-start.35
  183.2 2.2 collective-permute-done.35
  191.3 2.5 %collective-permute-done.37 = bf16[32,2048]{1,0:T(8,128)(2,1)S(1)} collective-permute-done((bf16[32,2048]{1,0:T(8,128)(2,1)S(1)}, bf16[32,2048]{1,0:T(8,128)(2,1)S(1)}, u32[]{:S(2)}, u32[]{:S(2)}) %collective-permute-start.37) | collective-permute-done | bytes 131104 | tf_op jit(solution)/shard_map/ppermute | solution.py:57
  195.2 3.2 %collective-permute-done.38 = bf16[32,2048]{1,0:T(8,128)(2,1)S(1)} collective-permute-done((bf16[32,2048]{1,0:T(8,128)(2,1)S(1)}, bf16[32,2048]{1,0:T(8,128)(2,1)S(1)}, u32[]{:S(2)}, u32[]{:S(2)}) %collective-permute-start.38) | collective-permute-done | bytes 131104 | tf_op jit(solution)/shard_map/ppermute | solution.py:57
  199.6 3.2 %collective-permute-done.39 = bf16[32,2048]{1,0:T(8,128)(2,1)S(1)} collective-permute-done((bf16[32,2048]{1,0:T(8,128)(2,1)S(1)}, bf16[32,2048]{1,0:T(8,128)(2,1)S(1)}, u32[]{:S(2)}, u32[]{:S(2)}) %collective-permute-start.39) | collective-permute-done | bytes 131104 | tf_op jit(solution)/shard_map/ppermute | solution.py:57
  202.8 2.2 collective-permute-start.40
  205.0 11.4 %collective-permute-start.34 = (bf16[64,2048]{1,0:T(8,128)(2,1)S(1)}, bf16[64,2048]{1,0:T(8,128)(2,1)S(1)}, u32[]{:S(2)}, u32[]{:S(2)}) collective-permute-start(bf16[64,2048]{1,0:T(8,128)(2,1)S(1)} %get-tuple-element.17), channel_id=1, source_target_pairs={{0,1},{1,0},{2,3},{3,2},{4,5},{5,4},{6,7},{7,6},{8,9},{9,8},{10,11... | collective-permute-start | bytes 786440 | tf_op jit(solution)/shard_map/ppermute | solution.py:47
  218.0 3.5 %collective-permute-done.33 = bf16[32,2048]{1,0:T(8,128)(2,1)S(1)} collective-permute-done((bf16[32,2048]{1,0:T(8,128)(2,1)S(1)}, bf16[32,2048]{1,0:T(8,128)(2,1)S(1)}, u32[]{:S(2)}, u32[]{:S(2)}) %collective-permute-start.33) | collective-permute-done | bytes 131104 | tf_op jit(solution)/shard_map/ppermute | solution.py:56
  221.6 5.8 %collective-permute-start.42 = (bf16[64,2048]{1,0:T(8,128)(2,1)S(1)}, bf16[64,2048]{1,0:T(8,128)(2,1)S(1)}, u32[]{:S(2)}, u32[]{:S(2)}) collective-permute-start(bf16[64,2048]{1,0:T(8,128)(2,1)S(1)} %pad_maximum_fusion.3), channel_id=1, source_target_pairs={{0,0},{1,16},{16,17},{17,1},{2,2},{3,18},{18,19},{19,3},{4,4},{5,2... | collective-permute-start | bytes 786440 | tf_op jit(solution)/shard_map/ppermute | solution.py:63
  227.4 3.3 %collective-permute-done.42 = bf16[64,2048]{1,0:T(8,128)(2,1)S(1)} collective-permute-done((bf16[64,2048]{1,0:T(8,128)(2,1)S(1)}, bf16[64,2048]{1,0:T(8,128)(2,1)S(1)}, u32[]{:S(2)}, u32[]{:S(2)}) %collective-permute-start.42) | collective-permute-done | bytes 262176 | tf_op jit(solution)/shard_map/ppermute | solution.py:63
  (157 shorter events, 61.9 us)
Async XLA Ops:
  1.9 9.2 %collective-permute-start = (bf16[72,2048]{1,0:T(8,128)(2,1)S(1)}, bf16[72,2048]{1,0:T(8,128)(2,1)S(1)}, u32[]{:S(2)}, u32[]{:S(2)}) collective-permute-start(bf16[72,2048]{1,0:T(8,128)(2,1)S(1)} %pad_maximum_fusion.2), channel_id=1, source_target_pairs={{0,0},{16,1},{17,16},{1,17},{2,2},{18,3},{19,18},{3,19},{4,4},{20,... | collective-permute-start | bytes 884744 | tf_op jit(solution)/shard_map/ppermute | solution.py:18
  11.1 5.6 %collective-permute-start.2 = (bf16[72,2048]{1,0:T(8,128)(2,1)S(1)}, bf16[72,2048]{1,0:T(8,128)(2,1)S(1)}, u32[]{:S(2)}, u32[]{:S(2)}) collective-permute-start(bf16[72,2048]{1,0:T(8,128)(2,1)S(1)} %collective-permute-done), channel_id=1, source_target_pairs={{0,4},{4,8},{8,12},{12,14},{14,10},{10,6},{6,2},{2,0},{1,5},{5,9},... | collective-permute-start | bytes 884744 | tf_op jit(solution)/shard_map/ppermute | solution.py:22
  12.4 5.6 %collective-permute-start.10 = (bf16[72,2048]{1,0:T(8,128)(2,1)S(1)}, bf16[72,2048]{1,0:T(8,128)(2,1)S(1)}, u32[]{:S(2)}, u32[]{:S(2)}) collective-permute-start(bf16[72,2048]{1,0:T(8,128)(2,1)S(1)} %collective-permute-done), channel_id=1, source_target_pairs={{4,0},{8,4},{12,8},{14,12},{10,14},{6,10},{2,6},{0,2},{5,1},{9,5},... | collective-permute-start | bytes 884744 | tf_op jit(solution)/shard_map/ppermute | solution.py:25
  12.5 6.7 %collective-permute-start.1 = (bf16[72,2048]{1,0:T(8,128)(2,1)S(1)}, bf16[72,2048]{1,0:T(8,128)(2,1)S(1)}, u32[]{:S(2)}, u32[]{:S(2)}) collective-permute-start(bf16[72,2048]{1,0:T(8,128)(2,1)S(1)} %collective-permute-done), channel_id=1, source_target_pairs={{0,1},{1,0},{2,3},{3,2},{4,5},{5,4},{6,7},{7,6},{8,9},{9,8},{10,11... | collective-permute-start | bytes 884744 | tf_op jit(solution)/shard_map/ppermute | solution.py:28
  16.7 10.9 %collective-permute-start.3 = (bf16[72,2048]{1,0:T(8,128)(2,1)S(1)}, bf16[72,2048]{1,0:T(8,128)(2,1)S(1)}, u32[]{:S(2)}, u32[]{:S(2)}) collective-permute-start(bf16[72,2048]{1,0:T(8,128)(2,1)S(1)} %collective-permute-done.2), channel_id=1, source_target_pairs={{0,1},{1,0},{2,3},{3,2},{4,5},{5,4},{6,7},{7,6},{8,9},{9,8},{10,11... | collective-permute-start | bytes 884744 | tf_op jit(solution)/shard_map/ppermute | solution.py:28
  16.7 8.1 %collective-permute-start.4 = (bf16[72,2048]{1,0:T(8,128)(2,1)S(1)}, bf16[72,2048]{1,0:T(8,128)(2,1)S(1)}, u32[]{:S(2)}, u32[]{:S(2)}) collective-permute-start(bf16[72,2048]{1,0:T(8,128)(2,1)S(1)} %collective-permute-done.2), channel_id=1, source_target_pairs={{0,4},{4,8},{8,12},{12,14},{14,10},{10,6},{6,2},{2,0},{1,5},{5,9},... | collective-permute-start | bytes 884744 | tf_op jit(solution)/shard_map/ppermute | solution.py:22
  18.0 9.4 %collective-permute-start.11 = (bf16[72,2048]{1,0:T(8,128)(2,1)S(1)}, bf16[72,2048]{1,0:T(8,128)(2,1)S(1)}, u32[]{:S(2)}, u32[]{:S(2)}) collective-permute-start(bf16[72,2048]{1,0:T(8,128)(2,1)S(1)} %collective-permute-done.10), channel_id=1, source_target_pairs={{4,0},{8,4},{12,8},{14,12},{10,14},{6,10},{2,6},{0,2},{5,1},{9,5},... | collective-permute-start | bytes 884744 | tf_op jit(solution)/shard_map/ppermute | solution.py:25
  18.1 28.4 %collective-permute-start.15 = (bf16[72,2048]{1,0:T(8,128)(2,1)S(1)}, bf16[72,2048]{1,0:T(8,128)(2,1)S(1)}, u32[]{:S(2)}, u32[]{:S(2)}) collective-permute-start(bf16[72,2048]{1,0:T(8,128)(2,1)S(1)} %collective-permute-done.10), channel_id=1, source_target_pairs={{0,1},{1,0},{2,3},{3,2},{4,5},{5,4},{6,7},{7,6},{8,9},{9,8},{10,11... | collective-permute-start | bytes 884744 | tf_op jit(solution)/shard_map/ppermute | solution.py:28
  24.7 10.8 %collective-permute-start.5 = (bf16[72,2048]{1,0:T(8,128)(2,1)S(1)}, bf16[72,2048]{1,0:T(8,128)(2,1)S(1)}, u32[]{:S(2)}, u32[]{:S(2)}) collective-permute-start(bf16[72,2048]{1,0:T(8,128)(2,1)S(1)} %collective-permute-done.4), channel_id=1, source_target_pairs={{0,1},{1,0},{2,3},{3,2},{4,5},{5,4},{6,7},{7,6},{8,9},{9,8},{10,11... | collective-permute-start | bytes 884744 | tf_op jit(solution)/shard_map/ppermute | solution.py:28
  26.1 8.6 %collective-permute-start.6 = (bf16[72,2048]{1,0:T(8,128)(2,1)S(1)}, bf16[72,2048]{1,0:T(8,128)(2,1)S(1)}, u32[]{:S(2)}, u32[]{:S(2)}) collective-permute-start(bf16[72,2048]{1,0:T(8,128)(2,1)S(1)} %collective-permute-done.4), channel_id=1, source_target_pairs={{0,4},{4,8},{8,12},{12,14},{14,10},{10,6},{6,2},{2,0},{1,5},{5,9},... | collective-permute-start | bytes 884744 | tf_op jit(solution)/shard_map/ppermute | solution.py:22
  27.4 9.4 %collective-permute-start.12 = (bf16[72,2048]{1,0:T(8,128)(2,1)S(1)}, bf16[72,2048]{1,0:T(8,128)(2,1)S(1)}, u32[]{:S(2)}, u32[]{:S(2)}) collective-permute-start(bf16[72,2048]{1,0:T(8,128)(2,1)S(1)} %collective-permute-done.11), channel_id=1, source_target_pairs={{4,0},{8,4},{12,8},{14,12},{10,14},{6,10},{2,6},{0,2},{5,1},{9,5},... | collective-permute-start | bytes 884744 | tf_op jit(solution)/shard_map/ppermute | solution.py:25
  27.6 18.8 %collective-permute-start.14 = (bf16[72,2048]{1,0:T(8,128)(2,1)S(1)}, bf16[72,2048]{1,0:T(8,128)(2,1)S(1)}, u32[]{:S(2)}, u32[]{:S(2)}) collective-permute-start(bf16[72,2048]{1,0:T(8,128)(2,1)S(1)} %collective-permute-done.11), channel_id=1, source_target_pairs={{0,1},{1,0},{2,3},{3,2},{4,5},{5,4},{6,7},{7,6},{8,9},{9,8},{10,11... | collective-permute-start | bytes 884744 | tf_op jit(solution)/shard_map/ppermute | solution.py:28
  34.6 10.3 %collective-permute-start.7 = (bf16[72,2048]{1,0:T(8,128)(2,1)S(1)}, bf16[72,2048]{1,0:T(8,128)(2,1)S(1)}, u32[]{:S(2)}, u32[]{:S(2)}) collective-permute-start(bf16[72,2048]{1,0:T(8,128)(2,1)S(1)} %collective-permute-done.6), channel_id=1, source_target_pairs={{0,1},{1,0},{2,3},{3,2},{4,5},{5,4},{6,7},{7,6},{8,9},{9,8},{10,11... | collective-permute-start | bytes 884744 | tf_op jit(solution)/shard_map/ppermute | solution.py:28
  35.5 8.6 %collective-permute-start.8 = (bf16[72,2048]{1,0:T(8,128)(2,1)S(1)}, bf16[72,2048]{1,0:T(8,128)(2,1)S(1)}, u32[]{:S(2)}, u32[]{:S(2)}) collective-permute-start(bf16[72,2048]{1,0:T(8,128)(2,1)S(1)} %collective-permute-done.6), channel_id=1, source_target_pairs={{0,4},{4,8},{8,12},{12,14},{14,10},{10,6},{6,2},{2,0},{1,5},{5,9},... | collective-permute-start | bytes 884744 | tf_op jit(solution)/shard_map/ppermute | solution.py:22
  36.8 9.4 %collective-permute-start.13 = (bf16[72,2048]{1,0:T(8,128)(2,1)S(1)}, bf16[72,2048]{1,0:T(8,128)(2,1)S(1)}, u32[]{:S(2)}, u32[]{:S(2)}) collective-permute-start(bf16[72,2048]{1,0:T(8,128)(2,1)S(1)} %collective-permute-done.12), channel_id=1, source_target_pairs={{0,1},{1,0},{2,3},{3,2},{4,5},{5,4},{6,7},{7,6},{8,9},{9,8},{10,11... | collective-permute-start | bytes 884744 | tf_op jit(solution)/shard_map/ppermute | solution.py:28
  60.0 30.1 %collective-permute-start.16 = (bf16[384,1536]{1,0:T(8,128)(2,1)}, bf16[384,1536]{1,0:T(8,128)(2,1)}, u32[]{:S(2)}, u32[]{:S(2)}) collective-permute-start(bf16[384,1536]{1,0:T(8,128)(2,1)} %pad_maximum_fusion), channel_id=1, source_target_pairs={{0,16},{16,0},{1,17},{17,1},{2,18},{18,2},{3,19},{19,3},{4,20},{20... | collective-permute-start | bytes 3538952 | tf_op jit(solution)/shard_map/ppermute | solution.py:171
  65.2 50.2 %collective-permute-start.17 = (bf16[384,1536]{1,0:T(8,128)(2,1)}, bf16[384,1536]{1,0:T(8,128)(2,1)}, u32[]{:S(2)}, u32[]{:S(2)}) collective-permute-start(bf16[384,1536]{1,0:T(8,128)(2,1)} %pad_maximum_fusion.1), channel_id=1, source_target_pairs={{0,16},{16,0},{1,17},{17,1},{2,18},{18,2},{3,19},{19,3},{4,20},{20... | collective-permute-start | bytes 3538952 | tf_op jit(solution)/shard_map/ppermute | solution.py:171
  94.0 33.9 %collective-permute-start.18 = (bf16[384,768]{1,0:T(8,128)(2,1)S(1)}, bf16[384,768]{1,0:T(8,128)(2,1)S(1)}, u32[]{:S(2)}, u32[]{:S(2)}) collective-permute-start(bf16[384,768]{1,0:T(8,128)(2,1)S(1)} %multiply_convert_fusion.1), channel_id=1, source_target_pairs={{0,16},{16,0},{1,17},{17,1},{2,18},{18,2},{3,19},{19,3},{4,20},{20... | collective-permute-start | bytes 1769480 | tf_op jit(solution)/shard_map/ppermute | solution.py:187
  118.2 22.3 %collective-permute-start.19 = (bf16[384,768]{1,0:T(8,128)(2,1)S(1)}, bf16[384,768]{1,0:T(8,128)(2,1)S(1)}, u32[]{:S(2)}, u32[]{:S(2)}) collective-permute-start(bf16[384,768]{1,0:T(8,128)(2,1)S(1)} %multiply_convert_fusion), channel_id=1, source_target_pairs={{0,16},{16,0},{1,17},{17,1},{2,18},{18,2},{3,19},{19,3},{4,20},{20... | collective-permute-start | bytes 1769480 | tf_op jit(solution)/shard_map/ppermute | solution.py:187
  154.3 6.3 %collective-permute-start.24 = (bf16[64,2048]{1,0:T(8,128)(2,1)S(1)}, bf16[64,2048]{1,0:T(8,128)(2,1)S(1)}, u32[]{:S(2)}, u32[]{:S(2)}) collective-permute-start(bf16[64,2048]{1,0:T(8,128)(2,1)S(1)} %get-tuple-element.22), channel_id=1, source_target_pairs={{0,1},{1,0},{2,3},{3,2},{4,5},{5,4},{6,7},{7,6},{8,9},{9,8},{10,11... | collective-permute-start | bytes 786440 | tf_op jit(solution)/shard_map/ppermute | solution.py:47
  159.1 6.6 %collective-permute-start.26 = (bf16[64,2048]{1,0:T(8,128)(2,1)S(1)}, bf16[64,2048]{1,0:T(8,128)(2,1)S(1)}, u32[]{:S(2)}, u32[]{:S(2)}) collective-permute-start(bf16[64,2048]{1,0:T(8,128)(2,1)S(1)} %get-tuple-element.21), channel_id=1, source_target_pairs={{0,1},{1,0},{2,3},{3,2},{4,5},{5,4},{6,7},{7,6},{8,9},{9,8},{10,11... | collective-permute-start | bytes 786440 | tf_op jit(solution)/shard_map/ppermute | solution.py:47
  163.0 7.9 %collective-permute-start.28 = (bf16[64,2048]{1,0:T(8,128)(2,1)S(1)}, bf16[64,2048]{1,0:T(8,128)(2,1)S(1)}, u32[]{:S(2)}, u32[]{:S(2)}) collective-permute-start(bf16[64,2048]{1,0:T(8,128)(2,1)S(1)} %get-tuple-element.20), channel_id=1, source_target_pairs={{0,1},{1,0},{2,3},{3,2},{4,5},{5,4},{6,7},{7,6},{8,9},{9,8},{10,11... | collective-permute-start | bytes 786440 | tf_op jit(solution)/shard_map/ppermute | solution.py:47
  165.8 5.2 %collective-permute-start.27 = (bf16[32,2048]{1,0:T(8,128)(2,1)S(1)}, bf16[32,2048]{1,0:T(8,128)(2,1)S(1)}, u32[]{:S(2)}, u32[]{:S(2)}) collective-permute-start(bf16[32,2048]{1,0:T(8,128)(2,1)S(1)} %fusion.72), channel_id=1, source_target_pairs={{0,4},{4,8},{8,12},{12,14},{14,10},{10,6},{6,2},{2,0},{1,5},{5,9},... | collective-permute-start | bytes 393224 | tf_op jit(solution)/shard_map/ppermute | solution.py:56
  167.1 9.1 %collective-permute-start.30 = (bf16[64,2048]{1,0:T(8,128)(2,1)S(1)}, bf16[64,2048]{1,0:T(8,128)(2,1)S(1)}, u32[]{:S(2)}, u32[]{:S(2)}) collective-permute-start(bf16[64,2048]{1,0:T(8,128)(2,1)S(1)} %get-tuple-element.19), channel_id=1, source_target_pairs={{0,1},{1,0},{2,3},{3,2},{4,5},{5,4},{6,7},{7,6},{8,9},{9,8},{10,11... | collective-permute-start | bytes 786440 | tf_op jit(solution)/shard_map/ppermute | solution.py:47
  171.0 5.2 %collective-permute-start.29 = (bf16[32,2048]{1,0:T(8,128)(2,1)S(1)}, bf16[32,2048]{1,0:T(8,128)(2,1)S(1)}, u32[]{:S(2)}, u32[]{:S(2)}) collective-permute-start(bf16[32,2048]{1,0:T(8,128)(2,1)S(1)} %fusion.70), channel_id=1, source_target_pairs={{0,4},{4,8},{8,12},{12,14},{14,10},{10,6},{6,2},{2,0},{1,5},{5,9},... | collective-permute-start | bytes 393224 | tf_op jit(solution)/shard_map/ppermute | solution.py:56
  172.3 5.2 %collective-permute-start.32 = (bf16[64,2048]{1,0:T(8,128)(2,1)S(1)}, bf16[64,2048]{1,0:T(8,128)(2,1)S(1)}, u32[]{:S(2)}, u32[]{:S(2)}) collective-permute-start(bf16[64,2048]{1,0:T(8,128)(2,1)S(1)} %get-tuple-element.18), channel_id=1, source_target_pairs={{0,1},{1,0},{2,3},{3,2},{4,5},{5,4},{6,7},{7,6},{8,9},{9,8},{10,11... | collective-permute-start | bytes 786440 | tf_op jit(solution)/shard_map/ppermute | solution.py:47
  176.3 4.8 %collective-permute-start.31 = (bf16[32,2048]{1,0:T(8,128)(2,1)S(1)}, bf16[32,2048]{1,0:T(8,128)(2,1)S(1)}, u32[]{:S(2)}, u32[]{:S(2)}) collective-permute-start(bf16[32,2048]{1,0:T(8,128)(2,1)S(1)} %fusion.68), channel_id=1, source_target_pairs={{0,4},{4,8},{8,12},{12,14},{14,10},{10,6},{6,2},{2,0},{1,5},{5,9},... | collective-permute-start | bytes 393224 | tf_op jit(solution)/shard_map/ppermute | solution.py:56
  202.8 13.6 %collective-permute-start.40 = (bf16[32,2048]{1,0:T(8,128)(2,1)S(1)}, bf16[32,2048]{1,0:T(8,128)(2,1)S(1)}, u32[]{:S(2)}, u32[]{:S(2)}) collective-permute-start(bf16[32,2048]{1,0:T(8,128)(2,1)S(1)} %fusion.53), channel_id=1, source_target_pairs={{4,0},{8,4},{12,8},{14,12},{10,14},{6,10},{2,6},{0,2},{5,1},{9,5},... | collective-permute-start | bytes 393224 | tf_op jit(solution)/shard_map/ppermute | solution.py:57
  205.0 13.0 %collective-permute-start.34 = (bf16[64,2048]{1,0:T(8,128)(2,1)S(1)}, bf16[64,2048]{1,0:T(8,128)(2,1)S(1)}, u32[]{:S(2)}, u32[]{:S(2)}) collective-permute-start(bf16[64,2048]{1,0:T(8,128)(2,1)S(1)} %get-tuple-element.17), channel_id=1, source_target_pairs={{0,1},{1,0},{2,3},{3,2},{4,5},{5,4},{6,7},{7,6},{8,9},{9,8},{10,11... | collective-permute-start | bytes 786440 | tf_op jit(solution)/shard_map/ppermute | solution.py:47
  216.4 5.1 %collective-permute-start.33 = (bf16[32,2048]{1,0:T(8,128)(2,1)S(1)}, bf16[32,2048]{1,0:T(8,128)(2,1)S(1)}, u32[]{:S(2)}, u32[]{:S(2)}) collective-permute-start(bf16[32,2048]{1,0:T(8,128)(2,1)S(1)} %get-tuple-element.15), channel_id=1, source_target_pairs={{0,4},{4,8},{8,12},{12,14},{14,10},{10,6},{6,2},{2,0},{1,5},{5,9},... | collective-permute-start | bytes 393224 | tf_op jit(solution)/shard_map/ppermute | solution.py:56
  216.5 5.0 %collective-permute-start.41 = (bf16[32,2048]{1,0:T(8,128)(2,1)S(1)}, bf16[32,2048]{1,0:T(8,128)(2,1)S(1)}, u32[]{:S(2)}, u32[]{:S(2)}) collective-permute-start(bf16[32,2048]{1,0:T(8,128)(2,1)S(1)} %fusion.51), channel_id=1, source_target_pairs={{4,0},{8,4},{12,8},{14,12},{10,14},{6,10},{2,6},{0,2},{5,1},{9,5},... | collective-permute-start | bytes 393224 | tf_op jit(solution)/shard_map/ppermute | solution.py:57
  221.6 9.1 %collective-permute-start.42 = (bf16[64,2048]{1,0:T(8,128)(2,1)S(1)}, bf16[64,2048]{1,0:T(8,128)(2,1)S(1)}, u32[]{:S(2)}, u32[]{:S(2)}) collective-permute-start(bf16[64,2048]{1,0:T(8,128)(2,1)S(1)} %pad_maximum_fusion.3), channel_id=1, source_target_pairs={{0,0},{1,16},{16,17},{17,1},{2,2},{3,18},{18,19},{19,3},{4,4},{5,2... | collective-permute-start | bytes 786440 | tf_op jit(solution)/shard_map/ppermute | solution.py:63
  (22 other events, 192.4 us)
